TPU v7x, 8 devices: a whole 2x2x1 slice. The times are simulated.
8 devices in a mesh: rows: 8 (over z, y, x, core).
Axes of the slice: x: 2, y: 2, z: 1, core: 2. Of those that a mesh axis runs over, the one named last changes fastest.
Arguments:
- a_mat: float32 [16384, 256], P('rows')
- b_mat: float32 [16384, 4], P('rows')
Outputs:
- output 1: float32 [16384, 256], P('rows')
- output 2: float32 [256, 256], replicated
- output 3: float32 [256, 4], replicated
All inputs are finite; a program needn't handle non-finite values.
Results may differ from a plain program's by a relative error of at most 0.001.
Values sent between devices are 32-bit elements.
A program may use at most 1 GiB of HBM per device.

v0:
```python
import jax
import jax.numpy as jnp
from jax import lax
from jax.sharding import PartitionSpec as P

FULL_PRECISION = lax.Precision.HIGHEST


def solution(mesh):
    def local_fn(a_blk, b_blk):
        rows_local, num_cols = a_blk.shape
        dev_index = lax.axis_index('rows')
        global_row = dev_index * rows_local + jnp.arange(rows_local)
        col_ids = jnp.arange(num_cols)

        def factor_step(col_idx, carry):
            work_mat, reflectors, tau_vec = carry
            column = lax.dynamic_index_in_dim(work_mat, col_idx, axis=1, keepdims=False)
            below_mask = global_row >= col_idx
            at_pivot = global_row == col_idx
            column = jnp.where(below_mask, column, 0.0)
            local_stats = jnp.stack([jnp.sum(column * column), jnp.sum(jnp.where(at_pivot, column, 0.0))])
            col_stats = lax.psum(local_stats, 'rows')
            norm_val = jnp.sqrt(col_stats[0])
            pivot_val = col_stats[1]
            beta_val = jnp.where(pivot_val >= 0.0, -norm_val, norm_val)
            reflector = jnp.where(at_pivot, 1.0, column / (pivot_val - beta_val))
            tau_val = (beta_val - pivot_val) / beta_val
            part_proj = jnp.dot(reflector, work_mat, precision=FULL_PRECISION, preferred_element_type=jnp.float32)
            row_proj = lax.psum(part_proj, 'rows')
            work_mat = work_mat - (tau_val * reflector)[:, None] * row_proj[None, :]
            reflectors = lax.dynamic_update_index_in_dim(reflectors, reflector, col_idx, 0)
            tau_vec = jnp.where(col_ids == col_idx, tau_val, tau_vec)
            return work_mat, reflectors, tau_vec

        init_state = (a_blk, jnp.zeros((num_cols, rows_local), jnp.float32), jnp.zeros((num_cols,), jnp.float32))
        work_mat, reflectors, tau_vec = lax.fori_loop(0, num_cols, factor_step, init_state)
        top_rows = jnp.triu(work_mat[:num_cols])
        r_full = lax.psum(jnp.where(dev_index == 0, top_rows, 0.0), 'rows')

        def form_step(step_idx, q_work):
            col_idx = num_cols - 1 - step_idx
            reflector = lax.dynamic_index_in_dim(reflectors, col_idx, axis=0, keepdims=False)
            tau_val = lax.dynamic_index_in_dim(tau_vec, col_idx, axis=0, keepdims=False)
            part_proj = jnp.dot(reflector, q_work, precision=FULL_PRECISION, preferred_element_type=jnp.float32)
            row_proj = lax.psum(part_proj, 'rows')
            return q_work - (tau_val * reflector)[:, None] * row_proj[None, :]

        eye_part = (global_row[:, None] == col_ids[None, :]).astype(jnp.float32)
        q_work = lax.fori_loop(0, num_cols, form_step, eye_part)
        diag_signs = jnp.sign(jnp.diagonal(r_full))
        q_blk = q_work * diag_signs[None, :]
        r_fac = r_full * diag_signs[:, None]
        part_c = jnp.einsum('rn,rk->nk', q_blk, b_blk, precision=FULL_PRECISION, preferred_element_type=jnp.float32)
        c_mat = lax.psum(part_c, 'rows')
        return q_blk, r_fac, c_mat

    return jax.shard_map(local_fn, mesh=mesh, in_specs=(P('rows', None), P('rows', None)), out_specs=(P('rows', None), P(), P()), check_vma=False)
```

profile of v0, /device:TPU:0, one launch (start us, length us, event | category | flops | bytes accessed | tf_op | source)
XLA Modules:
  0.0 21321.0 jit_solution(17593793429437511169)
XLA Ops:
  9.2 14345.6 %while.34 = (s32[]{:T(128)}, f32[2048,256]{0,1:T(8,128)S(1)}, f32[256,2048]{1,0:T(8,128)}, f32[256]{0:T(256)S(1)}, s32[]{:T(128)}, /*index=5*/s32[]{:T(128)}, f32[]{:T(128)}, s32[]{:T(128)}) while((s32[]{:T(128)}, f32[2048,256]{0,1:T(8,128)S(1)}, f32[256,2048]{1,0:T(8,128)}, f32[256]{0:T(256)S(1)}, s32[]{:T(128)}, ...), condition=%wide.region_5.6_spmd.clone, body=%wide.region_0.5_spmd.clone.sunk | while | flops 7390219 | bytes 6416673 | solution.py:37
  11.2 25.0 psum.58
  14358.8 6925.3 %while.33 = (s32[]{:T(128)}, f32[2048,256]{1,0:T(8,128)S(1)}, f32[256]{0:T(256)S(1)}, f32[256,2048]{1,0:T(8,128)}, s32[]{:T(128)}, /*index=5*/s32[]{:T(128)}, s32[]{:T(128)}, s32[]{:T(128)}) while((s32[]{:T(128)}, f32[2048,256]{1,0:T(8,128)S(1)}, f32[256]{0:T(256)S(1)}, f32[256,2048]{1,0:T(8,128)}, s32[]{:T(128)}, /*index=5*/s32[]{:T(128)}, ...), condition=%wide.region_8.9_spmd, body=%wide.region_6.8_spmd.sunk | while | flops 7342342 | bytes 6344855 | solution.py:50
  14416.0 24.0 psum.57
  14470.1 24.0 psum.57
  14524.2 24.0 psum.57
  14578.3 24.0 psum.57
  14632.4 24.0 psum.57
  14686.5 24.0 psum.57
  14740.6 24.0 psum.57
  14794.7 24.0 psum.57
  14848.8 24.0 psum.57
  14902.9 24.0 psum.57
  14957.0 24.0 psum.57
  15011.1 24.0 psum.57
  15065.2 24.0 psum.57
  15119.4 24.0 psum.57
  15173.5 24.0 psum.57
  15227.6 24.0 psum.57
  15281.7 24.0 psum.57
  15335.8 24.0 psum.57
  15389.9 24.0 psum.57
  15444.0 24.0 psum.57
  15498.1 24.0 psum.57
  15552.2 24.0 psum.57
  15606.3 24.0 psum.57
  15660.4 24.0 psum.57
  15714.5 24.0 psum.57
  15768.6 24.0 psum.57
  15822.7 24.0 psum.57
  15876.8 24.0 psum.57
  15930.9 24.0 psum.57
  16309.6 24.0 psum.57
  16580.1 24.0 psum.57
  16850.7 24.0 psum.57
  17337.6 24.0 psum.57
  17608.1 24.0 psum.57
  17878.6 24.0 psum.57
  18365.6 24.0 psum.57
  18636.1 24.0 psum.57
  18906.6 24.0 psum.57
  19393.5 24.0 psum.57
  19664.1 24.0 psum.57
  19934.6 24.0 psum.57
  20421.5 24.0 psum.57
  20692.0 24.0 psum.57
  20962.5 24.0 psum.57
  21289.3 24.0 psum.51
  (5098 shorter events, 19487.0 us)
Async XLA Ops:
  7.2 21281.0 %copy-start = (f32[2048,4]{0,1:T(4,128)S(1)}, f32[2048,4]{0,1:T(4,128)}, u32[]{:S(2)}) copy-start(f32[2048,4]{0,1:T(4,128)} %param.7) | copy-start | bytes 98308
  7.2 21277.0 %all-reduce.2.cloned.1.call-start = ((), (), s32[]{:S(2)}) async-start(), calls=%async_computation | async-start | bytes 524288 | tf_op jit(solution)/shard_map/psum | solution.py:39
  21286.9 1.3 copy-start.1
  21288.2 25.1 copy-start.2
Sparse Core Ops, SparseCore 0:
  14358.5 44.3 all-reduce.1
where the time goes:
time: 21500 us; the launch traced here: 21300 us
  blocking collectives  18100 us (84%)
  local copies, waits for them, and re-layouts  949 us (4%)
  other arithmetic  906 us (4%)
  loops' own time  716 us (3%)
  matrix products  679 us (3%)
    psum x256, blocking collectives, factor_step(): col_stats = lax.psum(local_stats, 'rows')  6130 us
    psum x256, blocking collectives, form_step(): row_proj = lax.psum(part_proj, 'rows')  6010 us
    psum x256, blocking collectives, factor_step(): row_proj = lax.psum(part_proj, 'rows')  5890 us
    another operation x1, loops' own time, local_fn(): lax.fori_loop(0, num_cols, factor_step, init_state)  706 us
    dot_general x256, matrix products, factor_step(): jnp.dot(reflector, work_mat, precision=FULL_PRECISION, preferred_element_...  440 us

commit v1 on v0

v1 whole, which is shorter than its diff:
```python
import functools

import jax
import jax.numpy as jnp
from jax import lax
from jax.experimental import pallas as pl
from jax.experimental.pallas import tpu as pltpu
from jax.sharding import PartitionSpec as P

HI = lax.Precision.HIGHEST
F32 = jnp.float32
VM = pl.BlockSpec(memory_space=pltpu.VMEM)


def dot(x, y, dx, dy):
    return lax.dot_general(x, y, (((dx,), (dy,)), ((), ())), precision=HI, preferred_element_type=F32)


def bcast_row(x, i):
    return jnp.broadcast_to(x[i:i + 1, :], (8, x.shape[1]))

def factor(w_ref, n, nb, w):
    row8 = lax.broadcasted_iota(jnp.int32, (8, 128), 0)
    nt = nb // 8
    for k in range(n // nb):
        r0 = k * nb
        l0 = r0 // 128 * 128
        l1 = n + pl.cdiv(r0 + nb, 128) * 128
        wide = l1 - l0
        reps = wide // 128
        pan = [w_ref[r0 + 8 * t:r0 + 8 * t + 8, l0:l1] for t in range(nt)]
        scale = [None] * nt
        for b in range(nb // w):
            c0 = r0 + b * w - l0
            t0 = b * w // 8
            cols = [[jnp.broadcast_to(pan[t][:, c0 + j:c0 + j + 1], (8, 128)) if t >= t0 else None
                     for t in range(nt)] for j in range(w)]
            for j in range(w):
                jj = b * w + j
                tj, sj = jj // 8, jj % 8
                piv = bcast_row(cols[j][tj], sj)
                inv = lax.rsqrt(piv)
                lcol = [cols[j][t] * inv if t >= tj else None for t in range(nt)]
                lmul = list(lcol)
                lmul[tj] = jnp.where(row8 > sj, lcol[tj], 0.0)
                scale[tj] = inv if scale[tj] is None else jnp.where(row8 >= sj, inv, scale[tj])
                for j2 in range(j + 1, w):
                    q = b * w + j2
                    u = bcast_row(lcol[q // 8], q % 8)
                    for t in range(q // 8, nt):
                        cols[j2][t] = cols[j2][t] - lmul[t] * u
                urow = bcast_row(pan[tj], sj) * jnp.concatenate([inv] * reps, axis=1)
                for t in range(tj, nt):
                    pan[t] = pan[t] - jnp.concatenate([lmul[t]] * reps, axis=1) * urow
        done = jnp.concatenate([pan[t] * jnp.concatenate([scale[t]] * reps, axis=1) for t in range(nt)], axis=0)
        w_ref[r0:r0 + nb, l0:l1] = done
        r1 = r0 + nb
        if r1 < n:
            a0 = r1 // 128 * 128
            tall = done[:, a0 - l0:n - l0].T
            for lo, hi in ((r1, r1 + nb), (r1 + nb, n)):
                if lo < hi:
                    w_ref[lo:hi, l0:l1] -= jnp.dot(tall[lo - a0:hi - a0], done, precision=HI, preferred_element_type=F32)


def chol_kernel(nb, w, g_ref, u_ref, li_ref, w_ref):
    n = g_ref.shape[0]
    row = lax.broadcasted_iota(jnp.int32, (n, n), 0)
    col = lax.broadcasted_iota(jnp.int32, (n, n), 1)
    w_ref[:, :n] = g_ref[...]
    w_ref[:, n:] = jnp.where(row == col, 1.0, 0.0)
    factor(w_ref, n, nb, w)
    u_ref[...] = jnp.where(row <= col, w_ref[:, :n], 0.0)
    li_ref[...] = jnp.where(row >= col, w_ref[:, n:], 0.0)


def chol_inv(g):
    n = g.shape[0]
    return pl.pallas_call(
        functools.partial(chol_kernel, 32, 16),
        out_shape=[jax.ShapeDtypeStruct((n, n), F32)] * 2,
        in_specs=[VM], out_specs=[VM] * 2,
        scratch_shapes=[pltpu.VMEM((n, 2 * n), F32)],
        name="chol_inv",
    )(g)


def finish_kernel(q1_ref, g_ref, u_ref, c1_ref, q_ref, r_ref, c_ref, phi_ref, x_ref):
    n = g_ref.shape[0]
    row = lax.broadcasted_iota(jnp.int32, (n, n), 0)
    col = lax.broadcasted_iota(jnp.int32, (n, n), 1)
    half = jnp.where(row < col, 1.0, jnp.where(row == col, 0.5, 0.0))
    eye = jnp.where(row == col, 1.0, 0.0)
    dev = g_ref[...] - eye
    size = jnp.sqrt(jnp.sum(dev * dev))
    trips = jnp.where(size < 0.02, 3, 7)
    phi_ref[...] = dev * half

    def refine(_, carry):
        phi = phi_ref[...]
        phi_ref[...] = (dev - dot(phi, phi, 0, 0)) * half
        return carry

    lax.fori_loop(0, trips, refine, 0)
    phi = phi_ref[...]
    x_ref[...] = eye - phi

    def invert(_, carry):
        x_ref[...] = eye - dot(phi_ref[...], x_ref[...], 1, 0)
        return carry

    lax.fori_loop(0, trips, invert, 0)
    x = x_ref[...]
    r_ref[...] = jnp.where(row <= col, u_ref[...] + dot(phi, u_ref[...], 1, 0), 0.0)
    c_ref[...] = dot(x, c1_ref[...], 0, 0)
    q_ref[...] = dot(q1_ref[...], x, 1, 0)


def finish(q1, g, u, c1):
    n = g.shape[0]
    return pl.pallas_call(
        finish_kernel,
        out_shape=[jax.ShapeDtypeStruct(q1.shape, F32), jax.ShapeDtypeStruct((n, n), F32), jax.ShapeDtypeStruct(c1.shape, F32)],
        in_specs=[VM] * 4, out_specs=[VM] * 3,
        scratch_shapes=[pltpu.VMEM((n, n), F32)] * 2,
        name="finish",
    )(q1, g, u, c1)


def solution(mesh):
    def gram(q_blk, b_blk):
        g = dot(q_blk, q_blk, 0, 0)
        c = dot(q_blk, b_blk, 0, 0)
        return lax.psum(g, "rows"), lax.psum(c, "rows")

    def local_fn(a_blk, b_blk):
        n = a_blk.shape[1]
        eye = jnp.eye(n, dtype=F32)
        g0, _ = gram(a_blk, b_blk)
        u1, li = chol_inv(g0)
        q1 = dot(a_blk, li, 1, 1)
        g1, c1 = gram(q1, b_blk)

        def far(state):
            it, _, _, g, _, _, _ = state
            dev = g - eye
            return jnp.logical_and(jnp.logical_not(jnp.sum(dev * dev) < 0.01), it < 8)

        def again(state):
            it, q, u, g, c, a, b = state
            first = it == 0
            q = jnp.where(first, a, q)
            u = jnp.where(first, eye, u)
            g, _ = gram(q, b)
            step, inv = chol_inv(g + (2e-6 * jnp.trace(g)) * eye)
            q = dot(q, inv, 1, 1)
            u = dot(step, u, 1, 0)
            g, c = gram(q, b)
            return it + 1, q, u, g, c, a, b

        _, q1, u1, g1, c1, _, _ = lax.while_loop(far, again, (jnp.int32(0), q1, u1, g1, c1, a_blk, b_blk))
        return tuple(finish(q1, g1, u1, c1))

    return jax.shard_map(local_fn, mesh=mesh, in_specs=(P("rows", None), P("rows", None)), out_specs=(P("rows", None), P(), P()), check_vma=False)
```

time: 21500 us -> 137 us (0.01)
  blocking collectives: 18100 us -> 22.3 us
  local copies, waits for them, and re-layouts: 949 us -> 6.3 us
  other arithmetic: 906 us -> 2.41 us
  loops' own time: 716 us -> 0.87 us
  matrix products: 679 us -> 15.3 us
    psum x769 -> x1, blocking collectives: 18100 us -> 22.3 us  [gram(): return (lax.psum(g, 'rows'), lax.psum(c, 'rows'))]
    another operation x2 -> x1, loops' own time: 716 us -> 0.87 us  [local_fn(): lax.while_loop(far, again, (jnp.int32(0), q1, u1, g1, c1, a_blk, b_blk))]
    dot_general x513 -> x4, matrix products: 679 us -> 15.3 us  [dot(): lax.dot_general(x, y, (((dx,), (dy,)), ((), ())), precision=HI, preferred...]
    dynamic_slice x768 -> x0, local copies, waits for them, and re-layouts: 386 us -> none  [the longest x256 218 us: form_step(): lax.dynamic_index_in_dim(reflectors, col_idx, axis=0, keepdims=False)]
    dynamic_update_slice x256 -> x0, local copies, waits for them, and re-layouts: 386 us -> none  [factor_step(): lax.dynamic_update_index_in_dim(reflectors, reflector, col_idx, 0)]
    another operation x256 -> x0, other arithmetic: 338 us -> none  [factor_step(): jnp.stack([jnp.sum(column * column), jnp.sum(jnp.where(at_pivot, column,...]
where the time goes in v1:
time: 137 us; the launch traced here: 136 us
  waiting for transfers between devices  59.2 us (43%)
  blocking collectives  22.3 us (16%)
  Pallas kernels  15.7 us (11%)
  matrix products  15.3 us (11%)
  between operations  14.1 us (10%)
  local copies, waits for them, and re-layouts  6.3 us (5%)
  other arithmetic  2.41 us (2%)
    psum x2, waiting for transfers between devices, gram(): return (lax.psum(g, 'rows'), lax.psum(c, 'rows'))  59.2 us
    psum x1, blocking collectives, gram(): return (lax.psum(g, 'rows'), lax.psum(c, 'rows'))  22.3 us
    dot_general x4, matrix products, dot(): lax.dot_general(x, y, (((dx,), (dy,)), ((), ())), precision=HI, preferred...  15.3 us
    pallas_call x1, Pallas kernels, chol_inv(): pl.pallas_call(functools.partial(chol_kernel, 32, 16), out_shape=[jax.Sha...  8.37 us
    pallas_call x1, Pallas kernels, finish(): pl.pallas_call(finish_kernel, out_shape=[jax.ShapeDtypeStruct(q1.shape, F...  7.34 us
    unnamed x7, local copies, waits for them, and re-layouts  3.26 us
  transfers between devices with their start and end apart: 2, of which 2 were waited for; matrix products, arithmetic and copies ran while one was open for 4% of the time, Pallas kernels for 0%

profile of v1, /device:TPU:0, one launch (start us, length us, event | category | flops | bytes accessed | tf_op | source)
XLA Modules:
  0.0 136.5 jit_solution(9847834439935516627)
XLA Ops:
  7.2 0.0 copy-start
  7.2 0.0 all-reduce.5.cloned.1.call-start
  7.2 6.5 %fusion.13 = f32[256,256]{1,0:T(8,128)} fusion(f32[2048,256]{1,0:T(8,128)} %param.4), kind=kOutput, calls=%fused_computation.17 | convolution fusion | flops 1610612736 | bytes 2359296 | tf_op jit(solution)/shard_map/dot_general | solution.py:16
  13.8 0.0 all-reduce.5.cloned.1.call-update
  13.8 0.2 all-reduce.7.cloned.1.call-start
  14.0 0.7 fusion.10
  14.7 44.6 %all-reduce.5.cloned.1.call-done.g_ref = f32[256,256]{1,0:T(8,128)} async-done(((f32[256,256]{1,0:T(8,128)}), f32[256,256]{1,0:T(8,128)}) %all-reduce.5.cloned.1.call-update) | async-done | bytes 262160 | tf_op jit(solution)/shard_map/psum | solution.py:134
  59.3 8.4 %chol_inv.2 = (f32[256,256]{1,0:T(8,128)S(1)}, f32[256,256]{1,0:T(8,128)}) custom-call(f32[256,256]{1,0:T(8,128)} %all-reduce.5.cloned.1.call-done.g_ref), custom_call_target="tpu_custom_call" | custom-call | tf_op jit(solution)/shard_map/chol_inv/pallas_call | solution.py:79
  67.7 0.0 copy-done
  67.7 2.9 %fusion.14 = f32[256,2048]{1,0:T(8,128)S(1)} fusion(f32[256,256]{1,0:T(8,128)} %get-tuple-element.58, f32[2048,256]{1,0:T(8,128)S(1)} %copy-done), kind=kOutput, calls=%fused_computation.18 | convolution fusion | flops 1610612736 | bytes 4456448 | tf_op jit(solution)/shard_map/dot_general | solution.py:16
  70.6 0.0 copy-start.1
  70.6 1.3 copy-done.1
  71.9 0.0 copy-start.4
  71.9 2.6 %fusion.15 = f32[256,256]{1,0:T(8,128)} fusion(f32[256,2048]{1,0:T(8,128)S(1)} %fusion.14), kind=kOutput, calls=%fused_computation.19 | convolution fusion | flops 1610612736 | bytes 2359296 | tf_op jit(solution)/shard_map/dot_general | solution.py:16
  74.5 0.0 all-reduce.7.cloned.1.call-update
  74.5 0.0 copy-done.4
  74.5 3.3 %fusion.16 = f32[256,4]{0,1:T(4,128)S(1)} fusion(f32[256,2048]{1,0:T(8,128)} %copy-done.1, f32[2048,4]{0,1:T(4,128)S(1)} %copy-done.4), kind=kOutput, calls=%fused_computation.20 | convolution fusion | flops 25165824 | bytes 2134016 | tf_op jit(solution)/shard_map/dot_general | solution.py:16
  77.8 1.9 %copy.5 = f32[2048,256]{1,0:T(8,128)S(1)} copy(f32[2048,256]{0,1:T(8,128)} %bitcast.27) | data formatting | bytes 4194304
  79.8 22.3 %psum.47 = f32[256,4]{0,1:T(4,128)} all-reduce(f32[256,4]{0,1:T(4,128)S(1)} %fusion.16), channel_id=1, replica_groups=mesh['rows'=8] {'rows'}, use_global_device_ids=true, to_apply=%region_2.0 | all-reduce | flops 1024 | bytes 8192 | tf_op jit(solution)/shard_map/psum | solution.py:134
  102.1 14.6 %all-reduce.7.cloned.1.call-done = f32[256,256]{1,0:T(8,128)} async-done(((f32[256,256]{1,0:T(8,128)}), f32[256,256]{1,0:T(8,128)}) %all-reduce.7.cloned.1.call-update) | async-done | bytes 262160 | tf_op jit(solution)/shard_map/psum | solution.py:134
  116.7 2.6 %while.17 = (s32[]{:T(128)}, f32[2048,256]{1,0:T(8,128)S(1)}, f32[256,256]{1,0:T(8,128)S(1)}, f32[256,256]{1,0:T(8,128)}, f32[256,4]{0,1:T(4,128)}, /*index=5*/f...) while((s32[]{:T(128)}, f32[2048,256]{1,0:T(8,128)S(1)}, ...), condition=%wide.region_8.10_spmd.clone, body=%wide.region_3.8_spmd.clone.sunk | while | flops 5060297728 | bytes 28094760 | solution.py:161
  116.7 1.7 %multiply_reduce_fusion.1 = f32[]{:T(128)} fusion(f32[256,256]{1,0:T(8,128)} %get-tuple-element.122, f32[256,256]{1,0:T(8,128)} %get-tuple-element.123), kind=kLoop, calls=%fused_computation.1.clone | loop fusion | flops 196607 | bytes 524292 | tf_op jit(solution)/shard_map/while/cond/reduce_sum | solution.py:147
  119.2 1.5 %copy.6.c1_ref = f32[256,4]{1,0:T(8,128)} copy(f32[256,4]{0,1:T(4,128)} %get-tuple-element.63) | data formatting | bytes 8192 | tf_op jit(solution)/shard_map/while | solution.py:161
  120.7 7.3 %finish.1 = (f32[2048,256]{1,0:T(8,128)}, f32[256,256]{1,0:T(8,128)}, f32[256,4]{1,0:T(8,128)}) custom-call(f32[2048,256]{1,0:T(8,128)S(1)} %get-tuple-element.60.q1_ref, f32[256,256]{1,0:T(8,128)} %get-tuple-element.61.g_ref, f32[256,256]{1,0:T(8,128)S(1)} %get-tuple-element.62.u_ref, f32[256,4]{1,0:T(8,128)} %copy.6.c1_ref), custom_call_target="tpu_custom_call" | custom-call | tf_op jit(solution)/shard_map/finish/pallas_call | solution.py:121
  128.1 1.6 %copy.7 = f32[256,4]{0,1:T(4,128)} copy(f32[256,4]{1,0:T(8,128)} %get-tuple-element.97) | data formatting | bytes 8192 | tf_op jit(solution)/shard_map/finish/pallas_call | solution.py:121
Async XLA Ops:
  7.2 60.5 %copy-start = (f32[2048,256]{1,0:T(8,128)S(1)}, f32[2048,256]{1,0:T(8,128)}, u32[]{:S(2)}) copy-start(f32[2048,256]{1,0:T(8,128)} %param.4) | copy-start | bytes 6291460
  7.2 52.1 %all-reduce.5.cloned.1.call-start = ((), (), s32[]{:S(2)}) async-start(), calls=%async_computation | async-start | bytes 524288 | tf_op jit(solution)/shard_map/psum | solution.py:134
  13.8 102.9 %all-reduce.7.cloned.1.call-start = ((), (), s32[]{:S(2)}) async-start(), calls=%async_computation.1 | async-start | bytes 524288 | tf_op jit(solution)/shard_map/psum | solution.py:134
  70.6 1.3 copy-start.1
  71.9 2.6 %copy-start.4 = (f32[2048,4]{0,1:T(4,128)S(1)}, f32[2048,4]{0,1:T(4,128)}, u32[]{:S(2)}) copy-start(f32[2048,4]{0,1:T(4,128)} %param.5) | copy-start | bytes 98308
Sparse Core Ops, SparseCore 0:
  13.9 45.3 all-reduce.4
  74.6 41.9 all-reduce.6

commit v2 on v1

--- a/solution.py
+++ b/solution.py
@@ -10,6 +10,12 @@
 HI = lax.Precision.HIGHEST
 F32 = jnp.float32
 VM = pl.BlockSpec(memory_space=pltpu.VMEM)
+ANY = pl.BlockSpec(memory_space=pl.ANY)
+SM = pl.BlockSpec(memory_space=pltpu.SMEM)
+MESH = pl.DeviceIdType.MESH
+CHUNK = 512
+PACK = 416
+HALF, QUARTER = PACK // 2, PACK // 4
 
 
 def dot(x, y, dx, dy):
@@ -63,37 +69,153 @@
                     w_ref[lo:hi, l0:l1] -= jnp.dot(tall[lo - a0:hi - a0], done, precision=HI, preferred_element_type=F32)
 
 
-def chol_kernel(nb, w, g_ref, u_ref, li_ref, w_ref):
-    n = g_ref.shape[0]
+def neighbours():
+    me = lax.axis_index("rows")
+    core, x, y = me % 2, me // 2 % 2, me // 4
+    return core, (me + 1 - 2 * core, me + 2 - 4 * x, me + 4 - 8 * y)
+
+
+def entry_barrier():
+    barrier = pltpu.get_barrier_semaphore()
+    for device in neighbours()[1]:
+        pl.semaphore_signal(barrier, inc=1, device_id=(device,), device_id_type=MESH)
+    pl.semaphore_wait(barrier, 3)
+
+
+def all_reduce(part, total, bufs, send, recv):
+    got0, mine1, got1, mine2, got2 = bufs
+    core, (mate, x_dev, y_dev) = neighbours()
+    keep = pl.multiple_of(core * HALF, 8)
+    give = pl.multiple_of((1 - core) * HALF, 8)
+
+    def copy(src, dst, k, device):
+        return pltpu.make_async_remote_copy(
+            src_ref=src, dst_ref=dst, send_sem=send.at[k], recv_sem=recv.at[k], device_id=(device,), device_id_type=MESH
+        )
+
+    c0 = copy(part.at[pl.ds(give, HALF)], got0, 0, mate)
+    c0.start()
+    c0.wait()
+    for q in range(2):
+        mine1[q] = part[pl.ds(pl.multiple_of(keep + q * QUARTER, 8), QUARTER)] + got0[q * QUARTER:(q + 1) * QUARTER]
+    step1 = [copy(mine1.at[q], got1.at[q], 1 + q, (x_dev, y_dev)[q]) for q in range(2)]
+    for c in step1:
+        c.start()
+    step2 = [copy(mine2.at[q], got2.at[q], 3 + q, (y_dev, x_dev)[q]) for q in range(2)]
+    for q in range(2):
+        step1[q].wait()
+        mine2[q] = mine1[q] + got1[q]
+        step2[q].start()
+    for q in range(2):
+        step2[q].wait()
+        total[pl.ds(pl.multiple_of(keep + q * QUARTER, 8), QUARTER)] = mine2[q] + got2[q]
+    c3 = copy(total.at[pl.ds(keep, HALF)], total.at[pl.ds(keep, HALF)], 5, mate)
+    c3.start()
+    c3.wait()
+
+
+def pack_gram(part, g):
+    part[0:128] = g[:128, :128]
+    part[128:256] = g[:128, 128:]
+    part[256:384] = g[128:, 128:]
+
+
+def unpack_gram(total):
+    top = jnp.concatenate([total[0:128], total[128:256]], axis=1)
+    low = jnp.concatenate([total[128:256].T, total[256:384]], axis=1)
+    return jnp.concatenate([top, low], axis=0)
+
+
+def front_kernel(a_ref, bt_ref, shift_ref, q_ref, u_ref, g_ref, ct_ref, size_ref,
+                 a_buf, q_buf, w_ref, x_ref, part, total, got0, mine1, got1, mine2, got2, a_sem, q_sem, send, recv):
+    n = a_ref.shape[1]
+    steps = a_ref.shape[0] // CHUNK
     row = lax.broadcasted_iota(jnp.int32, (n, n), 0)
     col = lax.broadcasted_iota(jnp.int32, (n, n), 1)
-    w_ref[:, :n] = g_ref[...]
+    loads = [pltpu.make_async_copy(a_ref.at[pl.ds(i * CHUNK, CHUNK)], a_buf.at[pl.ds(i * CHUNK, CHUNK)], a_sem.at[i])
+             for i in range(steps)]
+    for load in loads:
+        load.start()
+    entry_barrier()
+    g = None
+    for i in range(steps):
+        loads[i].wait()
+        blk = a_buf[i * CHUNK:(i + 1) * CHUNK]
+        add = dot(blk, blk, 0, 0)
+        g = add if g is None else g + add
+    part[0, 384:] = jnp.zeros((PACK - 384, 128), F32)
+    pack_gram(part.at[0], g)
+    sets = [tuple(r.at[k] for r in (got0, mine1, got1, mine2, got2)) for k in range(2)]
+    all_reduce(part.at[0], total.at[0], sets[0], send.at[0], recv.at[0])
+    g = unpack_gram(total.at[0])
+    w_ref[:, :n] = jnp.where(row == col, g * (1.0 + shift_ref[0, 0]), g)
     w_ref[:, n:] = jnp.where(row == col, 1.0, 0.0)
-    factor(w_ref, n, nb, w)
+    factor(w_ref, n, 32, 16)
     u_ref[...] = jnp.where(row <= col, w_ref[:, :n], 0.0)
-    li_ref[...] = jnp.where(row >= col, w_ref[:, n:], 0.0)
-
-
-def chol_inv(g):
-    n = g.shape[0]
+    x_ref[...] = jnp.where(row >= col, w_ref[:, n:], 0.0).T
+    x = x_ref[...]
+    g = ct = None
+    stores = []
+    for i in range(steps):
+        rows = pl.ds(i * CHUNK, CHUNK)
+        blk = dot(a_buf[rows], x, 1, 0)
+        q_buf[rows] = blk
+        store = pltpu.make_async_copy(q_buf.at[rows], q_ref.at[rows], q_sem.at[i])
+        store.start()
+        stores.append(store)
+        add = dot(blk, blk, 0, 0)
+        g = add if g is None else g + add
+        add = dot(bt_ref[:, rows], blk, 1, 0)
+        ct = add if ct is None else ct + add
+    part[1, 384:] = jnp.zeros((PACK - 384, 128), F32)
+    part[1, 384:388] = ct[:, :128]
+    part[1, 392:396] = ct[:, 128:]
+    pack_gram(part.at[1], g)
+    all_reduce(part.at[1], total.at[1], sets[1], send.at[1], recv.at[1])
+    g = unpack_gram(total.at[1])
+    g_ref[...] = g
+    ct_ref[...] = jnp.concatenate([total[1, 384:388], total[1, 392:396]], axis=1)
+    dev = jnp.where(row == col, g - 1.0, g)
+    size_ref[0, 0] = jnp.sum(dev * dev)
+    for store in stores:
+        store.wait()
+
+
+def front(a, bt, shift):
+    m, n = a.shape
+    k = bt.shape[0]
+    steps = m // CHUNK
+    quarters = pltpu.VMEM((2, 2, QUARTER, 128), F32)
     return pl.pallas_call(
-        functools.partial(chol_kernel, 32, 16),
-        out_shape=[jax.ShapeDtypeStruct((n, n), F32)] * 2,
-        in_specs=[VM], out_specs=[VM] * 2,
-        scratch_shapes=[pltpu.VMEM((n, 2 * n), F32)],
-        name="chol_inv",
-    )(g)
-
-
-def finish_kernel(q1_ref, g_ref, u_ref, c1_ref, q_ref, r_ref, c_ref, phi_ref, x_ref):
+        front_kernel,
+        out_shape=[jax.ShapeDtypeStruct((m, n), F32), jax.ShapeDtypeStruct((n, n), F32), jax.ShapeDtypeStruct((n, n), F32),
+                   jax.ShapeDtypeStruct((k, n), F32), jax.ShapeDtypeStruct((1, 1), F32)],
+        in_specs=[ANY, VM, SM], out_specs=[ANY, VM, VM, VM, SM],
+        scratch_shapes=[
+            pltpu.VMEM((m, n), F32), pltpu.VMEM((m, n), F32), pltpu.VMEM((n, 2 * n), F32), pltpu.VMEM((n, n), F32),
+            pltpu.VMEM((2, PACK, 128), F32), pltpu.VMEM((2, PACK, 128), F32), pltpu.VMEM((2, HALF, 128), F32),
+            quarters, quarters, quarters, quarters,
+            pltpu.SemaphoreType.DMA((steps,)), pltpu.SemaphoreType.DMA((steps,)),
+            pltpu.SemaphoreType.DMA((2, 6)), pltpu.SemaphoreType.DMA((2, 6)),
+        ],
+        compiler_params=pltpu.CompilerParams(collective_id=0, has_side_effects=True),
+        name="front",
+    )(a, bt, shift)
+
+
+def finish_kernel(q1_ref, g_ref, u_ref, ct_ref, size_ref, q_ref, r_ref, c_ref, phi_ref, x_ref, in_buf, out_buf, in_sem, out_sem):
     n = g_ref.shape[0]
+    steps = q1_ref.shape[0] // CHUNK
+    parts = [pl.ds(i * CHUNK, CHUNK) for i in range(steps)]
+    loads = [pltpu.make_async_copy(q1_ref.at[parts[i]], in_buf.at[parts[i]], in_sem.at[i]) for i in range(steps)]
+    for load in loads:
+        load.start()
     row = lax.broadcasted_iota(jnp.int32, (n, n), 0)
     col = lax.broadcasted_iota(jnp.int32, (n, n), 1)
     half = jnp.where(row < col, 1.0, jnp.where(row == col, 0.5, 0.0))
     eye = jnp.where(row == col, 1.0, 0.0)
     dev = g_ref[...] - eye
-    size = jnp.sqrt(jnp.sum(dev * dev))
-    trips = jnp.where(size < 0.02, 3, 7)
+    trips = jnp.where(size_ref[0, 0] < 4e-4, 3, 7)
     phi_ref[...] = dev * half
 
     def refine(_, carry):
@@ -111,54 +233,51 @@
 
     lax.fori_loop(0, trips, invert, 0)
     x = x_ref[...]
+    stores = []
+    for i in range(steps):
+        loads[i].wait()
+        out_buf[parts[i]] = dot(in_buf[parts[i]], x, 1, 0)
+        store = pltpu.make_async_copy(out_buf.at[parts[i]], q_ref.at[parts[i]], out_sem.at[i])
+        store.start()
+        stores.append(store)
     r_ref[...] = jnp.where(row <= col, u_ref[...] + dot(phi, u_ref[...], 1, 0), 0.0)
-    c_ref[...] = dot(x, c1_ref[...], 0, 0)
-    q_ref[...] = dot(q1_ref[...], x, 1, 0)
-
-
-def finish(q1, g, u, c1):
-    n = g.shape[0]
+    c_ref[...] = dot(ct_ref[...], x, 1, 0)
+    for store in stores:
+        store.wait()
+
+
+def finish(q1, g, u, ct, size):
+    m, n = q1.shape
+    steps = m // CHUNK
     return pl.pallas_call(
         finish_kernel,
-        out_shape=[jax.ShapeDtypeStruct(q1.shape, F32), jax.ShapeDtypeStruct((n, n), F32), jax.ShapeDtypeStruct(c1.shape, F32)],
-        in_specs=[VM] * 4, out_specs=[VM] * 3,
-        scratch_shapes=[pltpu.VMEM((n, n), F32)] * 2,
+        out_shape=[jax.ShapeDtypeStruct((m, n), F32), jax.ShapeDtypeStruct((n, n), F32), jax.ShapeDtypeStruct(ct.shape, F32)],
+        in_specs=[ANY, VM, VM, VM, SM], out_specs=[ANY, VM, VM],
+        scratch_shapes=[pltpu.VMEM((n, n), F32)] * 2 + [pltpu.VMEM((m, n), F32)] * 2 + [pltpu.SemaphoreType.DMA((steps,))] * 2,
         name="finish",
-    )(q1, g, u, c1)
+    )(q1, g, u, ct, size)
 
 
 def solution(mesh):
-    def gram(q_blk, b_blk):
-        g = dot(q_blk, q_blk, 0, 0)
-        c = dot(q_blk, b_blk, 0, 0)
-        return lax.psum(g, "rows"), lax.psum(c, "rows")
-
     def local_fn(a_blk, b_blk):
         n = a_blk.shape[1]
-        eye = jnp.eye(n, dtype=F32)
-        g0, _ = gram(a_blk, b_blk)
-        u1, li = chol_inv(g0)
-        q1 = dot(a_blk, li, 1, 1)
-        g1, c1 = gram(q1, b_blk)
+        bt = b_blk.T
+        q, u, g, ct, size = front(a_blk, bt, jnp.zeros((1, 1), F32))
 
         def far(state):
-            it, _, _, g, _, _, _ = state
-            dev = g - eye
-            return jnp.logical_and(jnp.logical_not(jnp.sum(dev * dev) < 0.01), it < 8)
+            it, _, _, _, _, size, _, _ = state
+            return jnp.logical_and(jnp.logical_not(size[0, 0] < 0.01), it < 8)
 
         def again(state):
-            it, q, u, g, c, a, b = state
+            it, q, u, _, _, _, a, bt = state
             first = it == 0
             q = jnp.where(first, a, q)
-            u = jnp.where(first, eye, u)
-            g, _ = gram(q, b)
-            step, inv = chol_inv(g + (2e-6 * jnp.trace(g)) * eye)
-            q = dot(q, inv, 1, 1)
-            u = dot(step, u, 1, 0)
-            g, c = gram(q, b)
-            return it + 1, q, u, g, c, a, b
-
-        _, q1, u1, g1, c1, _, _ = lax.while_loop(far, again, (jnp.int32(0), q1, u1, g1, c1, a_blk, b_blk))
-        return tuple(finish(q1, g1, u1, c1))
+            u = jnp.where(first, jnp.eye(n, dtype=F32), u)
+            q, step, g, ct, size = front(q, bt, jnp.full((1, 1), 1e-5, F32))
+            return it + 1, q, dot(step, u, 1, 0), g, ct, size, a, bt
+
+        _, q, u, g, ct, size, _, _ = lax.while_loop(far, again, (jnp.int32(0), q, u, g, ct, size, a_blk, bt))
+        q, r, c = finish(q, g, u, ct, size)
+        return q, r, c.T
 
     return jax.shard_map(local_fn, mesh=mesh, in_specs=(P("rows", None), P("rows", None)), out_specs=(P("rows", None), P(), P()), check_vma=False)

time: 137 us -> 50.5 us (0.37)
  waiting for transfers between devices: 59.2 us -> 0 us
  Pallas kernels: 15.7 us -> 48.5 us
  blocking collectives: 22.3 us -> 0 us
  matrix products: 15.3 us -> 0 us
  between operations: 14.1 us -> 0.86 us
  local copies, waits for them, and re-layouts: 6.3 us -> 0.01 us
  other arithmetic: 2.41 us -> 0 us
    psum x2 -> x0, waiting for transfers between devices: 59.2 us -> none  [gram(): return (lax.psum(g, 'rows'), lax.psum(c, 'rows'))]
    pallas_call x2, Pallas kernels: 15.7 us -> 48.5 us  [the longest x1 39 us: front(): pl.pallas_call(front_kernel, out_shape=[jax.ShapeDtypeStruct((m, n), F32)...]
    psum x1 -> x0, blocking collectives: 22.3 us -> none  [gram(): return (lax.psum(g, 'rows'), lax.psum(c, 'rows'))]
    dot_general x4 -> x0, matrix products: 15.3 us -> none  [dot(): lax.dot_general(x, y, (((dx,), (dy,)), ((), ())), precision=HI, preferred...]
    unnamed x7 -> x4, local copies, waits for them, and re-layouts: 3.26 us -> 0.01 us
    reduce_sum x1 -> x0, other arithmetic: 1.7 us -> none  [far(): return jnp.logical_and(jnp.logical_not(jnp.sum(dev * dev) < 0.01), it < 8)]
    pallas_call x1 -> x0, local copies, waits for them, and re-layouts: 1.58 us -> none  [finish(): pl.pallas_call(finish_kernel, out_shape=[jax.ShapeDtypeStruct(q1.shape, F...]
    while x1 -> x0, local copies, waits for them, and re-layouts: 1.46 us -> none  [local_fn(): lax.while_loop(far, again, (jnp.int32(0), q1, u1, g1, c1, a_blk, b_blk))]
  transfers between devices with their start and end apart: 2 -> 0, of which waited for: 2 -> 0; matrix products, arithmetic and copies ran while one was open for 4% -> 0% of each run, Pallas kernels for 0% -> 0%
where the time goes in v2:
time: 50.5 us; the launch traced here: 50.3 us
  Pallas kernels  48.5 us (96%)
  loops' own time  0.92 us (2%)
  between operations  0.86 us (2%)
    pallas_call x1, Pallas kernels, front(): pl.pallas_call(front_kernel, out_shape=[jax.ShapeDtypeStruct((m, n), F32)...  39 us
    pallas_call x1, Pallas kernels, finish(): pl.pallas_call(finish_kernel, out_shape=[jax.ShapeDtypeStruct((m, n), F32...  9.5 us

profile of v2, /device:TPU:0, one launch (start us, length us, event | category | flops | bytes accessed | tf_op | source)
XLA Modules:
  0.0 50.3 jit_solution(7663225559247633064)
XLA Ops:
  0.6 0.0 copy-start
  0.6 0.0 copy-start.1
  0.6 39.0 %front.2 = (f32[2048,256]{1,0:T(8,128)}, f32[256,256]{1,0:T(8,128)S(1)}, f32[256,256]{1,0:T(8,128)}, f32[4,256]{1,0:T(4,128)}, f32[1,1]{1,0:T(1,128)}) custom-call(f32[2048,256]{1,0:T(8,128)} %a_ref.1, f32[4,2048]{1,0:T(4,128)} %bitcast.7, f32[1,1]{1,0:T(1,128)} %constant.14.clone.1.shift_ref), custom_call_target="tpu_custom_call" | custom-call | tf_op jit(solution)/shard_map/front/pallas_call | solution.py:189
  39.7 0.0 copy-done
  39.7 0.0 copy-done.1
  39.7 0.9 %while.18 = (s32[]{:T(128)}, f32[2048,256]{1,0:T(8,128)}, f32[256,256]{1,0:T(8,128)S(1)}, f32[256,256]{1,0:T(8,128)}, f32[4,256]{1,0:T(4,128)}, /*index=5*/f32[1...) while((s32[]{:T(128)}, f32[2048,256]{1,0:T(8,128)}, ...), condition=%wide.region_1.2_spmd, body=%wide.region_0.1_spmd.sunk | while | flops 202047488 | bytes 7602310 | solution.py:279
  40.6 9.5 %finish.1 = (f32[2048,256]{1,0:T(8,128)}, f32[256,256]{1,0:T(8,128)}, f32[4,256]{1,0:T(4,128)}) custom-call(f32[2048,256]{1,0:T(8,128)} %get-tuple-element.65.q1_ref, f32[256,256]{1,0:T(8,128)} %get-tuple-element.66.g_ref, f32[256,256]{1,0:T(8,128)S(1)} %get-tuple-element.67.u_ref, f32[4,256]{1,0:T(4,128)} %get-tuple-element.68.ct_ref, ...), custom_call_target="tpu_custom_call" | custom-call | tf_op jit(solution)/shard_map/finish/pallas_call | solution.py:252
Async XLA Ops:
  0.6 39.1 %copy-start = (f32[2048,256]{1,0:T(8,128)S(1)}, f32[2048,256]{1,0:T(8,128)}, u32[]{:S(2)}) copy-start(f32[2048,256]{1,0:T(8,128)} %a_ref.1) | copy-start | bytes 6291460
  0.6 39.1 %copy-start.1 = (f32[2048,4]{0,1:T(4,128)S(1)}, f32[2048,4]{0,1:T(4,128)}, u32[]{:S(2)}) copy-start(f32[2048,4]{0,1:T(4,128)} %param.5) | copy-start | bytes 98308
